TPU v7x, 8 devices: a whole 2x2x1 slice. The times are simulated.
8 devices in a mesh: sys: 1 (over z), row: 8 (over y, x, core).
Axes of the slice: x: 2, y: 2, z: 1, core: 2. Of those that a mesh axis runs over, the one named last changes fastest.
Arguments:
- positions: bfloat16 [8192, 128], P(('sys', 'row'))
- charges: float32 [8192], P(('sys', 'row'))
- counts: int32 [8], P(('sys', 'row'))
Outputs:
- output 1: float32 [8192, 128], P(('sys', 'row'))
- output 2: float32 [1], P('sys')
All inputs are finite; a program needn't handle non-finite values.
Results may differ from a plain program's by a relative error of at most 0.001.
Values are sent between devices in bfloat16 or wider.
A program may use at most 1 GiB of HBM per device.

v0:
```python
import jax
import jax.numpy as jnp
from jax import lax
from jax.sharding import PartitionSpec as P


def sq_norm(block_pos):
    pos_f32 = block_pos.astype(jnp.float32)
    return jnp.sum(pos_f32 * pos_f32, axis=1)


def pair_weight(row_pos, row_q, col_pos, col_q, neg_scale):
    gram_mat = jnp.einsum('id,jd->ij', row_pos, col_pos, preferred_element_type=jnp.float32)
    dist_sq = jnp.maximum(sq_norm(row_pos)[:, None] + sq_norm(col_pos)[None, :] - 2.0 * gram_mat, 0.0)
    return row_q[:, None] * col_q[None, :] * jnp.exp(dist_sq * neg_scale)


def row_force(weight, w_low, row_pos, col_pos, inv_len2):
    pulled = jnp.dot(w_low, col_pos, preferred_element_type=jnp.float32)
    return (jnp.sum(weight, axis=1)[:, None] * row_pos.astype(jnp.float32) - pulled) * inv_len2


def col_force(weight, w_low, row_pos, col_pos, inv_len2):
    pushed = jnp.einsum('ij,id->jd', w_low, row_pos, preferred_element_type=jnp.float32)
    return (jnp.sum(weight, axis=0)[:, None] * col_pos.astype(jnp.float32) - pushed) * inv_len2


def solution(mesh):
    num_blocks = mesh.shape['row']
    half_way = num_blocks // 2
    next_perm = [(src, (src + 1) % num_blocks) for src in range(num_blocks)]
    home_perm = [(src, (src - half_way) % num_blocks) for src in range(num_blocks)]

    def per_device(positions, charges, counts):
        block_rows, width = positions.shape
        half_rows = block_rows // 2
        neg_scale = -0.5 / width
        inv_len2 = 1.0 / width
        live_q = jnp.where(jnp.arange(block_rows) < counts[0], charges, 0.0)
        diag_mask = jnp.arange(block_rows)[:, None] == jnp.arange(block_rows)[None, :]
        own_w = jnp.where(diag_mask, 0.0, pair_weight(positions, live_q, positions, live_q, neg_scale))
        own_force = row_force(own_w, own_w.astype(jnp.bfloat16), positions, positions, inv_len2)
        energy = 0.5 * jnp.sum(own_w)
        vis_pos = lax.ppermute(positions, 'row', next_perm)
        vis_q = lax.ppermute(live_q, 'row', next_perm)
        vis_react = jnp.zeros((block_rows, width), jnp.float32)

        def full_step(step_idx, loop_state):
            vis_pos, vis_q, vis_react, own_force, energy = loop_state
            weight = pair_weight(positions, live_q, vis_pos, vis_q, neg_scale)
            w_low = weight.astype(jnp.bfloat16)
            own_force = own_force + row_force(weight, w_low, positions, vis_pos, inv_len2)
            vis_react = vis_react + col_force(weight, w_low, positions, vis_pos, inv_len2)
            energy = energy + jnp.sum(weight)
            vis_pos = lax.ppermute(vis_pos, 'row', next_perm)
            vis_q = lax.ppermute(vis_q, 'row', next_perm)
            vis_react = lax.ppermute(vis_react, 'row', next_perm)
            return vis_pos, vis_q, vis_react, own_force, energy

        loop_state = lax.fori_loop(0, half_way - 1, full_step, (vis_pos, vis_q, vis_react, own_force, energy))
        vis_pos, vis_q, vis_react, own_force, energy = loop_state
        is_lower = lax.axis_index('row') < half_way
        a_pos = jnp.where(is_lower, positions[:half_rows], vis_pos[half_rows:])
        a_q = jnp.where(is_lower, live_q[:half_rows], vis_q[half_rows:])
        b_pos = jnp.where(is_lower, vis_pos, positions)
        b_q = jnp.where(is_lower, vis_q, live_q)
        weight = pair_weight(a_pos, a_q, b_pos, b_q, neg_scale)
        w_low = weight.astype(jnp.bfloat16)
        a_force = row_force(weight, w_low, a_pos, b_pos, inv_len2)
        b_force = col_force(weight, w_low, a_pos, b_pos, inv_len2)
        zero_half = jnp.zeros((half_rows, width), jnp.float32)
        own_force = own_force + jnp.where(is_lower, jnp.concatenate([a_force, zero_half], axis=0), b_force)
        vis_react = vis_react + jnp.where(is_lower, b_force, jnp.concatenate([zero_half, a_force], axis=0))
        energy = energy + jnp.sum(weight)
        own_force = own_force + lax.ppermute(vis_react, 'row', home_perm)
        energy = lax.psum(energy, 'row')
        return own_force, energy.reshape(1)

    row_spec = P(('sys', 'row'), None)
    vec_spec = P(('sys', 'row'))
    return jax.shard_map(per_device, mesh=mesh, in_specs=(row_spec, vec_spec, vec_spec), out_specs=(row_spec, P('sys')), check_vma=False)
```

profile of v0, /device:TPU:0, one launch (start us, length us, event | category | flops | bytes accessed | tf_op | source)
XLA Modules:
  0.0 96.8 jit_solution(6799004805963100611)
XLA Ops:
  1.3 0.7 fusion.23
  2.0 0.9 collective-permute-start.4
  2.8 2.6 %collective-permute-start.3 = (bf16[1024,128]{1,0:T(8,128)(2,1)}, bf16[1024,128]{1,0:T(8,128)(2,1)S(1)}, u32[]{:S(2)}, u32[]{:S(2)}) collective-permute-start(bf16[1024,128]{1,0:T(8,128)(2,1)} %param.5), channel_id=1, source_target_pairs={{0,1},{1,2},{2,3},{3,4},{4,5},{5,6},{6,7},{7,0}} | collective-permute-start | bytes 786440 | tf_op jit(solution)/shard_map/ppermute | solution.py:44
  5.4 1.2 %fusion.18 = f32[1024]{0:T(1024)S(1)} fusion(bf16[1024,128]{1,0:T(8,128)(2,1)} %param.5), kind=kLoop, calls=%fused_computation.30 | loop fusion | flops 392192 | bytes 266240 | tf_op jit(solution)/shard_map/reduce_sum | solution.py:9
  6.6 3.9 %fusion.25 = (f32[]{:T(128)}, f32[1024]{0:T(1024)S(1)}, bf16[1024,1024]{0,1:T(8,128)(2,1)S(1)}) fusion(bf16[1024,128]{1,0:T(8,128)(2,1)} %param.5, f32[1024]{0:T(1024)S(1)} %fusion.18, f32[1024]{0:T(1024)S(1)} %fusion.23), kind=kOutput, calls=%fused_computation.46 | convolution fusion | flops 281017344 | bytes 2371588 | tf_op jit(solution)/shard_map/id,jd->ij/dot_general | solution.py:13
  10.6 0.8 fusion.14
  12.1 50.7 %while.18 = (s32[]{:T(128)}, bf16[1024,128]{1,0:T(8,128)(2,1)S(1)}, f32[1024]{0:T(1024)S(1)}, f32[1024,128]{1,0:T(8,128)S(1)}, f32[1024,128]{1,0:T(8,128)S(1)}, ...) while((s32[]{:T(128)}, bf16[1024,128]{1,0:T(8,128)(2,1)S(1)}, ...), condition=%wide.region_9.10_spmd, body=%wide.region_3.9_spmd.sunk | while | flops 818933760 | bytes 14221541 | solution.py:60
  12.2 0.3 fusion.59
  12.5 3.4 %fusion.60 = (f32[]{:T(128)}, f32[1024]{0:T(1024)S(1)}, f32[1024]{0:T(1024)S(1)}, bf16[1024,1024]{1,0:T(8,128)(2,1)S(1)}) fusion(bf16[1024,128]{1,0:T(8,128)(2,1)S(1)} %get-tuple-element.183, bf16[1024,128]{1,0:T(8,128)(2,1)S(1)} %copy.12, f32[1024]{0:T(1024)S(1)} %get-tuple-element.152, f32[1024]{0:T(1024)S(1)} %get-tuple-element.153, ...), kind=kOutput, calls=%fused_computation.45.clone.1 | convolution fusion | flops 279967744 | bytes 2646020 | tf_op jit(solution)/shard_map/while/body/eval_jaxpr/id,jd->ij/dot_general | solution.py:13
  15.9 0.8 fusion.61
  16.7 1.6 %collective-permute-start = (bf16[1024,128]{1,0:T(8,128)(2,1)S(1)}, bf16[1024,128]{1,0:T(8,128)(2,1)S(1)}, u32[]{:S(2)}, u32[]{:S(2)}) collective-permute-start(bf16[1024,128]{1,0:T(8,128)(2,1)S(1)} %copy.12), channel_id=1, source_target_pairs={{0,1},{1,2},{2,3},{3,4},{4,5},{5,6},{6,7},{7,0}} | collective-permute-start | bytes 786440 | tf_op jit(solution)/shard_map/while/body/eval_jaxpr/ppermute | solution.py:55
  18.3 0.7 fusion.62
  19.7 9.3 %collective-permute-done.1 = f32[1024]{0:T(1024)S(1)} collective-permute-done((f32[1024]{0:T(1024)S(1)}, f32[1024]{0:T(1024)S(1)}, u32[]{:S(2)}, u32[]{:S(2)}) %collective-permute-start.1) | collective-permute-done | bytes 4128 | tf_op jit(solution)/shard_map/while/body/eval_jaxpr/ppermute | solution.py:56
  29.1 0.3 fusion.59
  29.4 3.4 %fusion.60 = (f32[]{:T(128)}, f32[1024]{0:T(1024)S(1)}, f32[1024]{0:T(1024)S(1)}, bf16[1024,1024]{1,0:T(8,128)(2,1)S(1)}) fusion(bf16[1024,128]{1,0:T(8,128)(2,1)S(1)} %get-tuple-element.183, bf16[1024,128]{1,0:T(8,128)(2,1)S(1)} %copy.12, f32[1024]{0:T(1024)S(1)} %get-tuple-element.152, f32[1024]{0:T(1024)S(1)} %get-tuple-element.153, ...), kind=kOutput, calls=%fused_computation.45.clone.1 | convolution fusion | flops 279967744 | bytes 2646020 | tf_op jit(solution)/shard_map/while/body/eval_jaxpr/id,jd->ij/dot_general | solution.py:13
  32.8 0.8 fusion.61
  33.6 0.7 collective-permute-start
  34.3 0.7 fusion.62
  35.8 10.2 %collective-permute-done.1 = f32[1024]{0:T(1024)S(1)} collective-permute-done((f32[1024]{0:T(1024)S(1)}, f32[1024]{0:T(1024)S(1)}, u32[]{:S(2)}, u32[]{:S(2)}) %collective-permute-start.1) | collective-permute-done | bytes 4128 | tf_op jit(solution)/shard_map/while/body/eval_jaxpr/ppermute | solution.py:56
  46.0 0.3 fusion.59
  46.3 3.4 %fusion.60 = (f32[]{:T(128)}, f32[1024]{0:T(1024)S(1)}, f32[1024]{0:T(1024)S(1)}, bf16[1024,1024]{1,0:T(8,128)(2,1)S(1)}) fusion(bf16[1024,128]{1,0:T(8,128)(2,1)S(1)} %get-tuple-element.183, bf16[1024,128]{1,0:T(8,128)(2,1)S(1)} %copy.12, f32[1024]{0:T(1024)S(1)} %get-tuple-element.152, f32[1024]{0:T(1024)S(1)} %get-tuple-element.153, ...), kind=kOutput, calls=%fused_computation.45.clone.1 | convolution fusion | flops 279967744 | bytes 2646020 | tf_op jit(solution)/shard_map/while/body/eval_jaxpr/id,jd->ij/dot_general | solution.py:13
  49.7 0.8 fusion.61
  50.6 0.7 fusion.62
  52.0 10.8 %collective-permute-done.1 = f32[1024]{0:T(1024)S(1)} collective-permute-done((f32[1024]{0:T(1024)S(1)}, f32[1024]{0:T(1024)S(1)}, u32[]{:S(2)}, u32[]{:S(2)}) %collective-permute-start.1) | collective-permute-done | bytes 4128 | tf_op jit(solution)/shard_map/while/body/eval_jaxpr/ppermute | solution.py:56
  62.8 0.2 fusion.19
  63.1 0.1 fusion.22
  63.2 1.9 %fusion.26 = (f32[]{:T(128)}, f32[1024]{0:T(1024)S(1)}, f32[512]{0:T(512)S(1)}, bf16[512,1024]{1,0:T(8,128)(2,1)S(1)}) fusion(bf16[512,128]{1,0:T(8,128)(2,1)S(1)} %get-tuple-element.78, bf16[1024,128]{1,0:T(8,128)(2,1)S(1)} %get-tuple-element.80, f32[1024]{0:T(1024)S(1)} %get-tuple-element.79, f32[512]{0:T(512)S(1)} %get-tuple-element.77, ...), kind=kOutput, calls=%fused_computation.47 | convolution fusion | flops 139983360 | bytes 1460228 | tf_op jit(solution)/shard_map/id,jd->ij/dot_general | solution.py:13
  65.1 0.4 fusion.17
  65.6 0.5 fusion.10
  66.1 1.5 %collective-permute-start.5 = (f32[1024,128]{1,0:T(8,128)S(1)}, f32[1024,128]{1,0:T(8,128)S(1)}, u32[]{:S(2)}, u32[]{:S(2)}) collective-permute-start(f32[1024,128]{1,0:T(8,128)S(1)} %select_add_fusion), channel_id=1, source_target_pairs={{0,4},{1,5},{2,6},{3,7},{4,0},{5,1},{6,2},{7,3}} | collective-permute-start | bytes 1572872 | tf_op jit(solution)/shard_map/ppermute | solution.py:75
  68.3 27.6 %psum.7 = f32[1]{0:T(128)} all-reduce(f32[1]{0:T(128)} %bitcast.1), channel_id=1, replica_groups=mesh['sys'=1,'row'=8] {'row'}, use_global_device_ids=true, to_apply=%region_15.16 | all-reduce | flops 1 | bytes 8 | tf_op jit(solution)/shard_map/psum | solution.py:76
  95.9 0.9 add_add_fusion
  (30 shorter events, 0.5 us)
Async XLA Ops:
  2.0 10.1 %collective-permute-start.4 = (f32[1024]{0:T(1024)S(1)}, f32[1024]{0:T(1024)S(1)}, u32[]{:S(2)}, u32[]{:S(2)}) collective-permute-start(f32[1024]{0:T(1024)S(1)} %fusion.23), channel_id=1, source_target_pairs={{0,1},{1,2},{2,3},{3,4},{4,5},{5,6},{6,7},{7,0}} | collective-permute-start | bytes 12296 | tf_op jit(solution)/shard_map/ppermute | solution.py:45
  2.8 9.2 %collective-permute-start.3 = (bf16[1024,128]{1,0:T(8,128)(2,1)}, bf16[1024,128]{1,0:T(8,128)(2,1)S(1)}, u32[]{:S(2)}, u32[]{:S(2)}) collective-permute-start(bf16[1024,128]{1,0:T(8,128)(2,1)} %param.5), channel_id=1, source_target_pairs={{0,1},{1,2},{2,3},{3,4},{4,5},{5,6},{6,7},{7,0}} | collective-permute-start | bytes 786440 | tf_op jit(solution)/shard_map/ppermute | solution.py:44
  6.6 4.0 %copy-start = (bf16[1024,128]{1,0:T(8,128)(2,1)S(1)}, bf16[1024,128]{1,0:T(8,128)(2,1)}, u32[]{:S(2)}) copy-start(bf16[1024,128]{1,0:T(8,128)(2,1)} %param.5) | copy-start | bytes 786436
  12.1 51.1 %copy-start.1 = (f32[1024]{0:T(1024)S(1)}, f32[1024]{0:T(1024)}, u32[]{:S(2)}) copy-start(f32[1024]{0:T(1024)} %param.6) | copy-start | bytes 12292
  16.6 12.4 %collective-permute-start.2 = (f32[1024,128]{1,0:T(8,128)S(1)}, f32[1024,128]{1,0:T(8,128)S(1)}, u32[]{:S(2)}, u32[]{:S(2)}) collective-permute-start(f32[1024,128]{1,0:T(8,128)S(1)} %fusion.61), channel_id=1, source_target_pairs={{0,1},{1,2},{2,3},{3,4},{4,5},{5,6},{6,7},{7,0}} | collective-permute-start | bytes 1572872 | tf_op jit(solution)/shard_map/while/body/eval_jaxpr/ppermute | solution.py:57
  16.7 12.3 %collective-permute-start = (bf16[1024,128]{1,0:T(8,128)(2,1)S(1)}, bf16[1024,128]{1,0:T(8,128)(2,1)S(1)}, u32[]{:S(2)}, u32[]{:S(2)}) collective-permute-start(bf16[1024,128]{1,0:T(8,128)(2,1)S(1)} %copy.12), channel_id=1, source_target_pairs={{0,1},{1,2},{2,3},{3,4},{4,5},{5,6},{6,7},{7,0}} | collective-permute-start | bytes 786440 | tf_op jit(solution)/shard_map/while/body/eval_jaxpr/ppermute | solution.py:55
  18.3 10.8 %collective-permute-start.1 = (f32[1024]{0:T(1024)S(1)}, f32[1024]{0:T(1024)S(1)}, u32[]{:S(2)}, u32[]{:S(2)}) collective-permute-start(f32[1024]{0:T(1024)S(1)} %copy.13), channel_id=1, source_target_pairs={{0,1},{1,2},{2,3},{3,4},{4,5},{5,6},{6,7},{7,0}} | collective-permute-start | bytes 12296 | tf_op jit(solution)/shard_map/while/body/eval_jaxpr/ppermute | solution.py:56
  33.5 12.4 %collective-permute-start.2 = (f32[1024,128]{1,0:T(8,128)S(1)}, f32[1024,128]{1,0:T(8,128)S(1)}, u32[]{:S(2)}, u32[]{:S(2)}) collective-permute-start(f32[1024,128]{1,0:T(8,128)S(1)} %fusion.61), channel_id=1, source_target_pairs={{0,1},{1,2},{2,3},{3,4},{4,5},{5,6},{6,7},{7,0}} | collective-permute-start | bytes 1572872 | tf_op jit(solution)/shard_map/while/body/eval_jaxpr/ppermute | solution.py:57
  33.6 12.3 %collective-permute-start = (bf16[1024,128]{1,0:T(8,128)(2,1)S(1)}, bf16[1024,128]{1,0:T(8,128)(2,1)S(1)}, u32[]{:S(2)}, u32[]{:S(2)}) collective-permute-start(bf16[1024,128]{1,0:T(8,128)(2,1)S(1)} %copy.12), channel_id=1, source_target_pairs={{0,1},{1,2},{2,3},{3,4},{4,5},{5,6},{6,7},{7,0}} | collective-permute-start | bytes 786440 | tf_op jit(solution)/shard_map/while/body/eval_jaxpr/ppermute | solution.py:55
  34.3 11.7 %collective-permute-start.1 = (f32[1024]{0:T(1024)S(1)}, f32[1024]{0:T(1024)S(1)}, u32[]{:S(2)}, u32[]{:S(2)}) collective-permute-start(f32[1024]{0:T(1024)S(1)} %copy.13), channel_id=1, source_target_pairs={{0,1},{1,2},{2,3},{3,4},{4,5},{5,6},{6,7},{7,0}} | collective-permute-start | bytes 12296 | tf_op jit(solution)/shard_map/while/body/eval_jaxpr/ppermute | solution.py:56
  50.5 12.4 %collective-permute-start.2 = (f32[1024,128]{1,0:T(8,128)S(1)}, f32[1024,128]{1,0:T(8,128)S(1)}, u32[]{:S(2)}, u32[]{:S(2)}) collective-permute-start(f32[1024,128]{1,0:T(8,128)S(1)} %fusion.61), channel_id=1, source_target_pairs={{0,1},{1,2},{2,3},{3,4},{4,5},{5,6},{6,7},{7,0}} | collective-permute-start | bytes 1572872 | tf_op jit(solution)/shard_map/while/body/eval_jaxpr/ppermute | solution.py:57
  50.5 12.3 %collective-permute-start = (bf16[1024,128]{1,0:T(8,128)(2,1)S(1)}, bf16[1024,128]{1,0:T(8,128)(2,1)S(1)}, u32[]{:S(2)}, u32[]{:S(2)}) collective-permute-start(bf16[1024,128]{1,0:T(8,128)(2,1)S(1)} %copy.12), channel_id=1, source_target_pairs={{0,1},{1,2},{2,3},{3,4},{4,5},{5,6},{6,7},{7,0}} | collective-permute-start | bytes 786440 | tf_op jit(solution)/shard_map/while/body/eval_jaxpr/ppermute | solution.py:55
  50.5 12.3 %collective-permute-start.1 = (f32[1024]{0:T(1024)S(1)}, f32[1024]{0:T(1024)S(1)}, u32[]{:S(2)}, u32[]{:S(2)}) collective-permute-start(f32[1024]{0:T(1024)S(1)} %copy.13), channel_id=1, source_target_pairs={{0,1},{1,2},{2,3},{3,4},{4,5},{5,6},{6,7},{7,0}} | collective-permute-start | bytes 12296 | tf_op jit(solution)/shard_map/while/body/eval_jaxpr/ppermute | solution.py:56
  66.1 29.8 %collective-permute-start.5 = (f32[1024,128]{1,0:T(8,128)S(1)}, f32[1024,128]{1,0:T(8,128)S(1)}, u32[]{:S(2)}, u32[]{:S(2)}) collective-permute-start(f32[1024,128]{1,0:T(8,128)S(1)} %select_add_fusion), channel_id=1, source_target_pairs={{0,4},{1,5},{2,6},{3,7},{4,0},{5,1},{6,2},{7,3}} | collective-permute-start | bytes 1572872 | tf_op jit(solution)/shard_map/ppermute | solution.py:75
where the time goes:
time: 97.1 us; the launch traced here: 96.8 us
  waiting for transfers between devices  30.3 us (31%)
  blocking collectives  27.6 us (28%)
  matrix products  22.1 us (23%)
  starting transfers between devices  7.5 us (8%)
  other arithmetic  4.2 us (4%)
  between operations  2.73 us (3%)
  loops' own time  2.24 us (2%)
    ppermute x3, waiting for transfers between devices, full_step(): vis_q = lax.ppermute(vis_q, 'row', next_perm)  30.3 us
    psum x1, blocking collectives, per_device(): energy = lax.psum(energy, 'row')  27.6 us
    dot_general x5, matrix products, pair_weight(): jnp.einsum('id,jd->ij', row_pos, col_pos, preferred_element_type=jnp.floa...  15.9 us
    dot_general x5, matrix products, row_force(): pulled = jnp.dot(w_low, col_pos, preferred_element_type=jnp.float32)  3.44 us
    dot_general x4, matrix products, col_force(): jnp.einsum('ij,id->jd', w_low, row_pos, preferred_element_type=jnp.float32)  2.8 us
    ppermute x1, starting transfers between devices, per_device(): vis_pos = lax.ppermute(positions, 'row', next_perm)  2.6 us
    reduce_sum x6, other arithmetic, sq_norm(): return jnp.sum(pos_f32 * pos_f32, axis=1)  2.55 us
    ppermute x3, starting transfers between devices, full_step(): vis_pos = lax.ppermute(vis_pos, 'row', next_perm)  2.3 us
  transfers between devices with their start and end apart: 12, of which 3 were waited for; matrix products, arithmetic and copies ran while one was open for 8% of the time, Pallas kernels for 0%

commit v1 on v0

v1 whole, which is shorter than its diff:
```python
import functools

import jax
import jax.numpy as jnp
from jax import lax
from jax.experimental import pallas as pl
from jax.experimental.pallas import tpu as pltpu
from jax.sharding import PartitionSpec as P

F32, BF16 = jnp.float32, jnp.bfloat16
LOG2E = 1.4426950408889634
NEG_BIG = -1e30
QUARTERS = 4
GROUPS = 6


def split3(val):
    hi = val.astype(BF16).astype(F32)
    rest = val - hi
    mid = rest.astype(BF16).astype(F32)
    low = (rest - mid).astype(BF16).astype(F32)
    return hi, mid, low


def kernel(cnt_ref, pos_hbm, q_ref, force_ref, energy_ref, xbuf, aux, xat, xai, lci, sacc, tacc, ebuf, load_sem,
           own_send, own_send_p, aux_send, aux_recv, fwd_send, ici_send, recv_p, recv_x, recv_y, prime_x, prime_y,
           e_send, e_recv):
    rows, width = pos_hbm.shape
    quarter = rows // QUARTERS
    lanes_per = quarter // 128
    me = lax.axis_index('row')
    core, ax, ay = me % 2, (me // 2) % 2, me // 4
    partner = me + 1 - 2 * core
    x_nbr = me + 2 - 4 * ax
    y_nbr = me + 4 - 8 * ay
    diag = x_nbr + 4 - 8 * ay
    off_p = 1 - 2 * core

    def rcopy(src, dst, send, recv, dev):
        return pltpu.make_async_remote_copy(src_ref=src, dst_ref=dst, send_sem=send, recv_sem=recv,
                                            device_id={'row': dev}, device_id_type=pl.DeviceIdType.MESH)

    def qref(blk, q):
        return xbuf.at[blk, pl.ds(q * quarter, quarter), :]

    load = pltpu.make_async_copy(pos_hbm, xbuf.at[me], load_sem)
    load.start()
    barrier = pltpu.get_barrier_semaphore()
    for dev in (partner, x_nbr, y_nbr):
        pl.semaphore_signal(barrier, inc=1, device_id={'row': dev}, device_id_type=pl.DeviceIdType.MESH)

    row_id = lax.broadcasted_iota(jnp.int32, (8, 128), 0) * 128 + lax.broadcasted_iota(jnp.int32, (8, 128), 1)
    live_q = jnp.where(row_id < cnt_ref[0], q_ref[...], 0.0)
    aux[me, 8:16, :] = live_q
    abs_q = jnp.abs(live_q)
    log_q = jnp.where(abs_q > 0.0, jnp.log(jnp.where(abs_q > 0.0, abs_q, 1.0)) * float(width), NEG_BIG)
    sacc[...] = jnp.zeros_like(sacc)
    tacc[...] = jnp.zeros_like(tacc)
    xat[...] = jnp.zeros_like(xat)
    load.wait()
    half_sq = []
    for grp in range(rows // 128):
        xt = jnp.transpose(xbuf[me, grp * 128:(grp + 1) * 128, :].astype(F32))
        half_sq.append(-0.5 * jnp.sum(xt * xt, axis=0, keepdims=True))
    half_sq = jnp.concatenate(half_sq, axis=0)
    aux[me, 0:8, :] = half_sq
    hi, mid, low = split3(half_sq + log_q)
    sub = lax.broadcasted_iota(jnp.int32, (128, 128), 0)
    for grp in range(rows // 128):
        sl = slice(grp * 128, (grp + 1) * 128)
        xai[sl, 0:width] = xbuf[me, sl, :]
        piece = jnp.where(sub == 0, hi[grp:grp + 1], jnp.where(sub == 1, mid[grp:grp + 1], jnp.where(
            sub == 2, low[grp:grp + 1], jnp.where(sub < 6, 1.0, 0.0))))
        xai[sl, width:2 * width] = jnp.transpose(piece).astype(BF16)
        lci[sl, :] = jnp.transpose(jnp.broadcast_to(log_q[grp:grp + 1], (128, 128)))

    pl.semaphore_wait(barrier, 3)

    sends = []
    for slot, dev in enumerate((partner, x_nbr, y_nbr)):
        cp = rcopy(aux.at[me], aux.at[me], aux_send.at[slot], aux_recv.at[slot], dev)
        cp.start()
        sends.append(cp)
    cp = rcopy(xbuf.at[me], xbuf.at[me], own_send_p, recv_p, partner)
    cp.start()
    sends.append(cp)
    for k in range(QUARTERS):
        cp = rcopy(qref(me, k), qref(me, k), own_send.at[0, k], recv_x.at[k], x_nbr)
        cp.start()
        sends.append(cp)
        qy = (k + 2) % QUARTERS
        cp = rcopy(qref(me, qy), qref(me, qy), own_send.at[1, k], recv_y.at[k], y_nbr)
        cp.start()
        sends.append(cp)

    def compute(blk_a, q_a, blk_b, q_b, own_half=None):
        chunk = 2 * quarter
        sub16 = lax.broadcasted_iota(jnp.int32, (16, quarter), 0)
        col_q = []
        xjs = []
        for side, (blk, q) in enumerate(((blk_a, q_a), (blk_b, q_b))):
            cs = slice(side * quarter, (side + 1) * quarter)
            xj = xbuf[blk, pl.ds(q * quarter, quarter), :]
            xjs.append(xj)
            xat[0:width, cs] = jnp.transpose(xj)
            srow = jnp.concatenate([aux[blk, pl.ds(q * lanes_per + t, 1), :] for t in range(lanes_per)], axis=1)
            col_q.append(jnp.concatenate(
                [aux[blk, pl.ds(8 + q * lanes_per + t, 1), :] for t in range(lanes_per)], axis=1))
            h, m, l = split3(srow)
            piece = jnp.where(sub16 < 3, 1.0, jnp.where(sub16 == 3, h, jnp.where(
                sub16 == 4, m, jnp.where(sub16 == 5, l, 0.0))))
            xat[width:width + 16, cs] = piece.astype(BF16)
        col_q = jnp.concatenate(col_q, axis=1)
        tile = 256
        for it in range(rows // tile):
            sl = slice(it * tile, (it + 1) * tile)
            gram = jnp.dot(xai[sl, :], xat[...], preferred_element_type=F32)
            cap = lci[sl, :]
            cap = jnp.concatenate([cap] * (chunk // 128), axis=1)
            weight = jnp.exp2(jnp.minimum(gram, cap) * (LOG2E / width)) * col_q
            if own_half is not None and own_half * chunk <= it * tile < (own_half + 1) * chunk:
                ri = lax.broadcasted_iota(jnp.int32, (tile, chunk), 0) + (it * tile - own_half * chunk)
                ci = lax.broadcasted_iota(jnp.int32, (tile, chunk), 1)
                weight = jnp.where(ri == ci, 0.0, weight)
            part = sacc[sl, :]
            for t in range(chunk // 128):
                part = part + weight[:, t * 128:(t + 1) * 128]
            sacc[sl, :] = part
            w_low = weight.astype(BF16)
            if VARIANT == 'a':
                tacc[sl, :] += jnp.dot(w_low[:, :quarter], xjs[0], preferred_element_type=F32) + jnp.dot(
                    w_low[:, quarter:], xjs[1], preferred_element_type=F32)
            else:
                tacc[:, sl] += lax.dot_general(xat[0:width, :], w_low, (((1,), (1,)), ((), ())),
                                               preferred_element_type=F32)

    compute(me, 0, me, 1, own_half=0)
    compute(me, 2, me, 3, own_half=1)
    rcopy(aux.at[partner], aux.at[partner], aux_send.at[0], aux_recv.at[0], partner).wait_recv()
    rcopy(xbuf.at[partner], xbuf.at[partner], own_send_p, recv_p, partner).wait_recv()

    @pl.loop(0, 2)
    def _(h):
        compute(partner, 2 * h, partner, 2 * h + 1)

    def aux_fwd(k_in, blk, slot, targets):
        rcopy(aux.at[blk], aux.at[blk], aux_send.at[0], aux_recv.at[k_in], partner).wait_recv()
        for n, (dev, k_out) in enumerate(targets):
            cp = rcopy(aux.at[blk], aux.at[blk], aux_send.at[slot + n], aux_recv.at[k_out], dev)
            cp.start()
            sends.append(cp)

    aux_fwd(1, x_nbr, 3, ((y_nbr, 3), (partner, 4)))
    aux_fwd(2, y_nbr, 5, ((partner, 5),))
    aux_fwd(3, diag, 6, ((partner, 6),))
    for k_in, blk in ((4, x_nbr), (5, y_nbr), (6, diag)):
        rcopy(aux.at[blk + off_p], aux.at[blk + off_p], aux_send.at[0], aux_recv.at[k_in], partner).wait_recv()

    @pl.loop(0, GROUPS)
    def _(k):
        far = k // QUARTERS
        blk_x = x_nbr + far * (diag - x_nbr)
        blk_y = y_nbr + far * (diag - y_nbr)
        q_x, q_y = k % QUARTERS, (k + 2) % QUARTERS
        src_x, src_y = qref(blk_x, q_x), qref(blk_y, q_y)
        rcopy(src_x, src_x, fwd_send.at[0, k], recv_x.at[k], partner).wait_recv()
        rcopy(src_x, src_x, fwd_send.at[0, k], prime_x.at[k], partner).start()

        @pl.when(k < 2)
        def _():
            rcopy(src_x, src_x, ici_send.at[0, k], recv_x.at[k + QUARTERS], y_nbr).start()

        rcopy(src_y, src_y, fwd_send.at[1, k], recv_y.at[k], partner).wait_recv()
        rcopy(src_y, src_y, fwd_send.at[1, k], prime_y.at[k], partner).start()

        @pl.when(k < 2)
        def _():
            rcopy(src_y, src_y, ici_send.at[1, k], recv_y.at[k + QUARTERS], x_nbr).start()

        @pl.loop(0, 2)
        def _(prime):
            bx, by = blk_x + prime * off_p, blk_y + prime * off_p
            px, py = qref(bx, q_x), qref(by, q_y)

            @pl.when(prime == 1)
            def _():
                rcopy(px, px, fwd_send.at[0, k], prime_x.at[k], partner).wait_recv()
                rcopy(py, py, fwd_send.at[1, k], prime_y.at[k], partner).wait_recv()

            compute(bx, q_x, by, q_y)

    total = jnp.zeros((8, 128), F32)
    live_q = aux[me, 8:16, :]
    sign = jnp.where(live_q < 0.0, -1.0, 1.0)
    for grp in range(rows // 128):
        sl = slice(grp * 128, (grp + 1) * 128)
        sign_col = jnp.transpose(jnp.broadcast_to(sign[grp:grp + 1], (128, 128)))
        row_sum = jnp.sum(sacc[sl, :], axis=1, keepdims=True)
        pulled = tacc[sl, :] if VARIANT == 'a' else jnp.transpose(tacc[:, sl])
        force_ref[sl, :] = (row_sum * xbuf[me, sl, :].astype(F32) - pulled) * (sign_col * (1.0 / width))
        signed = sacc[sl, :] * sign_col
        for t in range(16):
            total = total + signed[t * 8:(t + 1) * 8, :]
    ebuf[me] = total
    for n in range(1, 8):
        dev = (me + n) % 8
        cp = rcopy(ebuf.at[me], ebuf.at[me], e_send.at[n - 1], e_recv.at[n - 1], dev)
        cp.start()
        sends.append(cp)
    for cp in sends:
        cp.wait_send()

    @pl.loop(0, GROUPS)
    def _(k):
        for s in range(2):
            rcopy(qref(me, 0), qref(me, 0), fwd_send.at[s, k], prime_x.at[k], partner).wait_send()

    @pl.loop(0, 2)
    def _(k):
        for s in range(2):
            rcopy(qref(me, 0), qref(me, 0), ici_send.at[s, k], recv_x.at[k], partner).wait_send()

    for n in range(1, 8):
        src = (me + 8 - n) % 8
        rcopy(ebuf.at[src], ebuf.at[src], e_send.at[n - 1], e_recv.at[n - 1], src).wait_recv()
    energy_ref[0] = 0.5 * jnp.sum(jnp.sum(ebuf[...], axis=0))


VARIANT = 'b'


def solution(mesh):
    def per_device(positions, charges, counts):
        rows, width = positions.shape
        dma = pltpu.SemaphoreType.DMA
        tshape = (rows, width) if VARIANT == 'a' else (width, rows)
        forces, energy = pl.pallas_call(
            kernel,
            out_shape=(jax.ShapeDtypeStruct((rows, width), F32), jax.ShapeDtypeStruct((1,), F32)),
            in_specs=[pl.BlockSpec(memory_space=pltpu.SMEM), pl.BlockSpec(memory_space=pl.ANY),
                      pl.BlockSpec(memory_space=pltpu.VMEM)],
            out_specs=(pl.BlockSpec(memory_space=pltpu.VMEM), pl.BlockSpec(memory_space=pltpu.SMEM)),
            scratch_shapes=[
                pltpu.VMEM((8, rows, width), BF16),
                pltpu.VMEM((8, 16, 128), F32),
                pltpu.VMEM((2 * width, rows // 2), BF16),
                pltpu.VMEM((rows, 2 * width), BF16),
                pltpu.VMEM((rows, 128), F32),
                pltpu.VMEM((rows, 128), F32),
                pltpu.VMEM(tshape, F32),
                pltpu.VMEM((8, 8, 128), F32),
                dma, dma((2, QUARTERS)), dma, dma((7,)), dma((7,)), dma((2, GROUPS)), dma((2, 2)), dma,
                dma((GROUPS,)), dma((GROUPS,)), dma((GROUPS,)), dma((GROUPS,)), dma((7,)), dma((7,)),
            ],
            compiler_params=pltpu.CompilerParams(collective_id=0, has_side_effects=True),
        )(counts, positions, charges.reshape(8, 128))
        return forces, energy

    row_spec = P(('sys', 'row'), None)
    vec_spec = P(('sys', 'row'))
    return jax.shard_map(per_device, mesh=mesh, in_specs=(row_spec, vec_spec, vec_spec), out_specs=(row_spec, P('sys')),
                         check_vma=False)
```

time: 97.1 us -> 36.2 us (0.37)
  Pallas kernels: 0 us -> 31.1 us
  waiting for transfers between devices: 30.3 us -> 0 us
  blocking collectives: 27.6 us -> 0 us
  matrix products: 22.1 us -> 0 us
  starting transfers between devices: 7.5 us -> 0 us
  other arithmetic: 4.2 us -> 0 us
  loops' own time: 2.24 us -> 0 us
  local copies, waits for them, and re-layouts: 0.11 us -> 1.87 us
    pallas_call x0 -> x1, Pallas kernels: none -> 31.1 us  [per_device(): pl.pallas_call(kernel, out_shape=(jax.ShapeDtypeStruct((rows, width), F32...]
    ppermute x12 -> x0, waiting for transfers between devices: 30.3 us -> none  [the longest x3 30.3 us: full_step(): vis_q = lax.ppermute(vis_q, 'row', next_perm)]
    psum x1 -> x0, blocking collectives: 27.6 us -> none  [per_device(): energy = lax.psum(energy, 'row')]
    dot_general x14 -> x0, matrix products: 22.1 us -> none  [the longest x5 15.9 us: pair_weight(): jnp.einsum('id,jd->ij', row_pos, col_pos, preferred_element_type=jnp.floa...]
    ppermute x12 -> x0, starting transfers between devices: 7.5 us -> none  [the longest x1 2.6 us: per_device(): vis_pos = lax.ppermute(positions, 'row', next_perm)]
    reduce_sum x6 -> x0, other arithmetic: 2.55 us -> none  [sq_norm(): return jnp.sum(pos_f32 * pos_f32, axis=1)]
    another operation x1 -> x0, loops' own time: 2.24 us -> none  [per_device(): lax.fori_loop(0, half_way - 1, full_step, (vis_pos, vis_q, vis_react, own...]
    unnamed x4 -> x1, local copies, waits for them, and re-layouts: 0.01 us -> 1.87 us
  transfers between devices with their start and end apart: 12 -> 0, of which waited for: 3 -> 0; matrix products, arithmetic and copies ran while one was open for 8% -> 0% of each run, Pallas kernels for 0% -> 0%
where the time goes in v1:
time: 36.2 us; the launch traced here: 36 us
  Pallas kernels  31.1 us (86%)
  between operations  2.98 us (8%)
  local copies, waits for them, and re-layouts  1.87 us (5%)
    pallas_call x1, Pallas kernels, per_device(): pl.pallas_call(kernel, out_shape=(jax.ShapeDtypeStruct((rows, width), F32...  31.1 us
    unnamed x1, local copies, waits for them, and re-layouts  1.87 us

profile of v1, /device:TPU:0, one launch (start us, length us, event | category | flops | bytes accessed | tf_op | source)
XLA Modules:
  0.0 36.0 jit_solution(360744969152014648)
XLA Ops:
  1.3 31.1 %shard_map.50 = (f32[1024,128]{1,0:T(8,128)}, f32[1]{0:T(128)}) custom-call(s32[1]{0:T(128)S(6)} %copy.7.cnt_ref, bf16[1024,128]{1,0:T(8,128)(2,1)} %pos_hbm.1, f32[8,128]{1,0:T(8,128)} %bitcast.1), custom_call_target="tpu_custom_call" | custom-call | tf_op jit(solution)/shard_map/pallas_call | solution.py:237
  32.4 1.9 %copy.8 = f32[1024,128]{1,0:T(8,128)} copy(f32[1024,128]{1,0:T(8,128)} %get-tuple-element.4) | data formatting | bytes 1048576
